TPU v7x, 32 devices: a whole 2x2x4 slice. The times are simulated.
32 devices in a mesh: left: 8 (over y, x, core), right: 4 (over z).
Axes of the slice: x: 2, y: 2, z: 4, core: 2. Of those that a mesh axis runs over, the one named last changes fastest.
Arguments:
- signal: float32 [256, 256, 1024], P(None, 'left', 'right'), may hold values from -6 to 6
- symbol_x: float32 [256], replicated, may hold values from 0.3 to 3
- symbol_y: float32 [256], replicated, may hold values from 0.3 to 3
- symbol_z: float32 [1024], replicated, may hold values from 0.3 to 3
Outputs:
- spectrum: float32 [128, 128, 512], P('left', 'right')
All inputs are finite; a program needn't handle non-finite values.
Results may differ from a plain program's by a relative error of at most 0.000096.
Values sent between devices are 32-bit elements; how exact they have to be, the bound alone decides.
A program may use at most 128 MiB of HBM per device.

v0:
```python
import jax
import jax.numpy as jnp
from jax import lax
from jax.sharding import PartitionSpec as P


def transform_table(count):
    rank = jnp.arange(count)
    angle = (
        jnp.pi
        / (4 * count)
        * ((2 * rank[:, None] + 1) * (2 * rank[None, :] + 1) % (8 * count)).astype(jnp.float32)
    )
    return jnp.cos(angle) * (2.0 / count) ** 0.5


def transform_dim(values, dim):
    moved = jnp.tensordot(
        values,
        transform_table(values.shape[dim]),
        axes=([dim], [0]),
        precision=lax.Precision.HIGHEST,
    )
    return jnp.moveaxis(moved, -1, dim)


def body(signal, symbol_x, symbol_y, symbol_z):
    part_values = signal
    part_values = transform_dim(part_values, 0)
    part_values = lax.slice_in_dim(part_values, 0, part_values.shape[0] // 2, axis=0)
    part_values = lax.all_to_all(part_values, "left", split_axis=0, concat_axis=1, tiled=True)
    part_values = transform_dim(part_values, 1)
    pencil_values = lax.slice_in_dim(part_values, 0, part_values.shape[1] // 2, axis=1)
    pencil_values = lax.all_to_all(pencil_values, "right", split_axis=1, concat_axis=2, tiled=True)
    pencil_values = transform_dim(pencil_values, 2)
    pencil_values = lax.slice_in_dim(pencil_values, 0, pencil_values.shape[2] // 2, axis=2)
    share_x = pencil_values.shape[0]
    part_x = lax.dynamic_slice_in_dim(symbol_x, lax.axis_index("left") * share_x, share_x)
    share_y = pencil_values.shape[1]
    part_y = lax.dynamic_slice_in_dim(symbol_y, lax.axis_index("right") * share_y, share_y)
    symbol = (
        part_x[:, None, None]
        + part_y[None, :, None]
        + symbol_z[: pencil_values.shape[2]][None, None, :]
    )
    pencil_values = pencil_values * ((1.0 - 0.2 * symbol) / (1.0 + 0.2 * symbol))
    return pencil_values


def solution(mesh):
    in_specs = (P(None, "left", "right"), P(), P(), P())
    out_specs = P("left", "right", None)
    return jax.shard_map(body, mesh=mesh, in_specs=in_specs, out_specs=out_specs, check_vma=False)
```

profile of v0, /device:TPU:0, one launch (start us, length us, event | category | flops | bytes accessed | tf_op | source)
XLA Modules:
  0.0 144.7 jit_solution(14525953596823520953)
XLA Ops:
  0.0 1.0 fusion.17
  1.0 13.0 %fusion = f32[128,32,256]{2,0,1:T(8,128)S(1)} fusion(f32[256,32,256]{2,1,0:T(8,128)} %param.4, f32[256,256,1]{1,0,2:T(8,128)S(1)} %fusion.17), kind=kOutput, calls=%fused_computation | convolution fusion | flops 3221225472 | bytes 12713984 | tf_op jit(solution)/shard_map/dot_general | solution.py:18
  14.1 2.4 %copy.24 = f32[128,32,256]{2,1,0:T(8,128)S(1)} copy(f32[128,32,256]{2,0,1:T(8,128)S(1)} %fusion) | data formatting | bytes 8388608 | tf_op jit(solution)/shard_map/slice | solution.py:30
  16.5 54.0 %all_to_all.36 = f32[128,32,256]{2,1,0:T(8,128)S(1)} all-to-all(f32[128,32,256]{2,1,0:T(8,128)S(1)} %copy.24), channel_id=1, replica_groups=mesh['left'=8,'right'=4] {'left'}, dimensions={0} | all-to-all | bytes 8388608 | tf_op jit(solution)/shard_map/all_to_all | solution.py:31
  70.5 0.6 copy.25
  71.1 7.6 %convolution_bitcast_fusion = f32[16,256,256]{1,2,0:T(8,128)S(1)} fusion(f32[16,256,256]{2,1,0:T(8,128)S(1)} %bitcast.17, s32[256]{0:T(256)S(1)} %multiply_add_fusion.1), kind=kOutput, calls=%fused_computation.13 | convolution fusion | flops 3222208512 | bytes 8389632 | tf_op jit(solution)/shard_map/dot_general | solution.py:18
  78.7 0.2 slice.19
  78.9 0.0 copy-start
  78.9 0.0 copy-start.1
  78.9 2.1 %copy.27 = f32[16,128,256]{2,0,1:T(8,128)} copy(f32[16,128,256]{1,2,0:T(8,128)S(1)} %slice.19) | data formatting | bytes 4194304 | tf_op jit(solution)/shard_map/slice | solution.py:33
  81.0 4.9 %all-to-all-start.1 = ((f32[16,128,256]{2,0,1:T(8,128)}), f32[16,128,256]{2,0,1:T(8,128)S(1)}, u32[]{:S(2)}, u32[]{:S(2)}) async-start(f32[16,128,256]{2,0,1:T(8,128)} %copy.27), calls=%async_computation.1 | async-start | bytes 4194304 | tf_op jit(solution)/shard_map/all_to_all | solution.py:34
  85.8 0.0 copy-done
  85.8 0.1 dynamic_slice.7
  85.9 0.0 copy-done.1
  85.9 0.1 dynamic_slice.6
  86.0 0.1 broadcast_add_fusion
  86.1 16.7 %fusion.6 = f32[1024,1024,1]{1,0,2:T(8,128)} fusion(s32[1024]{0:T(1024)S(1)} %multiply_add_fusion), kind=kLoop, calls=%fused_computation.11 | loop fusion | flops 15728640 | bytes 4198400 | tf_op jit(solution)/shard_map/mul | solution.py:14
  102.8 30.7 %all-to-all-done.1 = f32[16,128,256]{2,0,1:T(8,128)S(1)} async-done(((f32[16,128,256]{2,0,1:T(8,128)}), f32[16,128,256]{2,0,1:T(8,128)S(1)}, u32[]{:S(2)}, u32[]{:S(2)}) %all-to-all-start.1) | async-done | bytes 2097184 | tf_op jit(solution)/shard_map/all_to_all | solution.py:34
  133.5 0.0 slice-start
  133.5 2.7 %copy.29 = f32[16,32,4,256]{3,2,1,0:T(4,128)} copy(f32[16,32,4,256]{3,0,1,2:T(8,128)S(1)} %bitcast.19) | data formatting | bytes 4194304 | tf_op jit(solution)/shard_map/all_to_all | solution.py:34
  136.2 2.3 %all_to_all.33 = f32[16,32,1024]{2,1,0:T(8,128)S(1)} reshape(f32[16,32,4,256]{3,2,1,0:T(4,128)} %copy.29) | data formatting | bytes 4194304 | tf_op jit(solution)/shard_map/all_to_all | solution.py:34
  138.5 0.0 slice-done
  138.5 6.2 %fusion.10 = f32[16,32,512]{2,1,0:T(8,128)} fusion(f32[16,32,1024]{2,1,0:T(8,128)S(1)} %all_to_all.33, f32[1024,1024,1]{1,0,2:T(8,128)} %fusion.6, f32[512]{0:T(512)S(1)} %slice-done, f32[16,32]{1,0:T(8,128)S(1)} %broadcast_add_fusion), kind=kOutput, calls=%fused_computation.16 | convolution fusion | flops 3222798336 | bytes 5246976 | tf_op jit(solution)/shard_map/dot_general | solution.py:18
  (2 shorter events, 0.0 us)
Async XLA Ops:
  78.9 7.0 %copy-start = (f32[256]{0:T(256)S(1)}, f32[256]{0:T(256)}, u32[]{:S(2)}) copy-start(f32[256]{0:T(256)} %param.6) | copy-start | bytes 3076
  78.9 7.0 %copy-start.1 = (f32[256]{0:T(256)S(1)}, f32[256]{0:T(256)}, u32[]{:S(2)}) copy-start(f32[256]{0:T(256)} %param.5) | copy-start | bytes 3076
  81.0 52.5 %all-to-all-start.1 = ((f32[16,128,256]{2,0,1:T(8,128)}), f32[16,128,256]{2,0,1:T(8,128)S(1)}, u32[]{:S(2)}, u32[]{:S(2)}) async-start(f32[16,128,256]{2,0,1:T(8,128)} %copy.27), calls=%async_computation.1 | async-start | bytes 4194304 | tf_op jit(solution)/shard_map/all_to_all | solution.py:34
  133.5 5.0 %slice-start = ((f32[1024]{0:T(1024)}), f32[512]{0:T(512)S(1)}, s32[]{:S(2)}) async-start(f32[1024]{0:T(1024)} %param.7), calls=%async_computation.2 | async-start | bytes 4096 | tf_op jit(solution)/shard_map/slice | solution.py:44
where the time goes:
time: 145 us
  blocking collectives  54 us (37%)
  waiting for transfers between devices  30.7 us (21%)
  matrix products  26.8 us (18%)
  other arithmetic  17.8 us (12%)
  local copies, waits for them, and re-layouts  10.4 us (7%)
  starting transfers between devices  4.87 us (3%)
    all_to_all x1, blocking collectives, body(): lax.all_to_all(part_values, 'left', split_axis=0, concat_axis=1, tiled=True)  54 us
    all_to_all x1, waiting for transfers between devices, body(): lax.all_to_all(pencil_values, 'right', split_axis=1, concat_axis=2, tiled...  30.7 us
    dot_general x3, matrix products, transform_dim(): jnp.tensordot(values, transform_table(values.shape[dim]), axes=([dim], [0...  26.8 us
    mul x2, other arithmetic, transform_table(): return jnp.cos(angle) * (2.0 / count) ** 0.5  17.7 us
    all_to_all x2, local copies, waits for them, and re-layouts, body(): lax.all_to_all(pencil_values, 'right', split_axis=1, concat_axis=2, tiled...  5 us
    all_to_all x1, starting transfers between devices, body(): lax.all_to_all(pencil_values, 'right', split_axis=1, concat_axis=2, tiled...  4.87 us
  transfers between devices with their start and end apart: 1, of which 1 were waited for; matrix products, arithmetic and copies ran while one was open for 12% of the time, Pallas kernels for 0%

commit v1 on v0

v1 whole, which is shorter than its diff:
```python
import functools

import jax
import jax.numpy as jnp
import numpy as np
from jax import lax
from jax.experimental import pallas as pl
from jax.experimental.pallas import tpu as pltpu
from jax.sharding import PartitionSpec as P

MESH = pl.DeviceIdType.MESH
LANES = 128
ROWS = 8
LAG = 2


def kept_table(count):
    rank = np.arange(count)
    odd = 2 * rank + 1
    angle = np.pi / (4 * count) * ((odd[:, None] * odd[None, : count // 2]) % (8 * count))
    return np.cos(angle) * (2.0 / count) ** 0.5


def two_halves(table):
    high = table.astype(np.float32).astype(jnp.bfloat16)
    rest = table - high.astype(np.float64)
    return np.stack([high, rest.astype(np.float32).astype(jnp.bfloat16)])


def split(values):
    high = values.astype(jnp.bfloat16)
    return high, (values - high.astype(jnp.float32)).astype(jnp.bfloat16)


def product(first, second):
    dot = functools.partial(jnp.dot, preferred_element_type=jnp.float32)
    return dot(first[0], second[0]) + (dot(first[0], second[1]) + dot(first[1], second[0]))


def kernel(
    lefts, rights, chunks,
    signal, table_x, table_y, table_z, symbol_x, symbol_y, symbol_z, out,
    held, tx, ty, tz, first, lines, second, pencils,
    held_sem, table_sem, send1, recv1, send2, recv2,
):
    left, right = lax.axis_index("left"), lax.axis_index("right")
    tiles, blocks, size_x = held.shape[0], held.shape[1], held.shape[2]
    modes_x, own_y = first.shape[1], first.shape[2]
    share_x, size_y = lines.shape[1], lines.shape[2]
    share_y = size_y // 2 // rights
    step = share_x // chunks
    width = blocks * LANES

    def tile_copy(t, b):
        return pltpu.make_async_copy(
            signal.at[:, pl.ds(t * ROWS, ROWS), pl.ds(b * LANES, LANES)],
            held.at[t, b], held_sem.at[t, b])

    copy_x = pltpu.make_async_copy(table_x, tx, table_sem.at[0])
    copy_y = pltpu.make_async_copy(table_y, ty, table_sem.at[1])
    copy_z = pltpu.make_async_copy(table_z, tz, table_sem.at[2])
    copy_x.start()
    for t in range(tiles):
        for b in range(blocks):
            tile_copy(t, b).start()
    copy_y.start()
    copy_z.start()

    barrier = pltpu.get_barrier_semaphore()
    for o in range(1, lefts):
        pl.semaphore_signal(barrier, 1, device_id=(lax.rem(left + o, lefts), right), device_id_type=MESH)
    for o in range(1, rights):
        pl.semaphore_signal(barrier, 1, device_id=(left, lax.rem(right + o, rights)), device_id_type=MESH)

    copy_x.wait()

    def stage1(t, carry):
        for b in range(blocks):
            tile_copy(t, b).wait()
        for y in range(ROWS):
            values = jnp.concatenate(
                [held.at[t, b].reshape(size_x * ROWS, LANES)[pl.ds(y, size_x, stride=ROWS), :] for b in range(blocks)],
                axis=1)
            result = product((tx[0], tx[1]), split(values))
            for b in range(blocks):
                first.at[b].reshape(modes_x * own_y, LANES)[pl.ds(t * ROWS + y, modes_x, stride=own_y), :] = (
                    result[:, b * LANES : (b + 1) * LANES])
        return carry

    lax.fori_loop(0, tiles, stage1, 0)
    pl.semaphore_wait(barrier, lefts + rights - 2)

    def send_left(c, o):
        to = lax.rem(left + o, lefts)
        return pltpu.make_async_remote_copy(
            src_ref=first.at[:, pl.ds(to * share_x + c * step, step)],
            dst_ref=lines.at[:, pl.ds(c * step, step), pl.ds(pl.multiple_of(left * own_y, own_y), own_y), :],
            send_sem=send1.at[o, c], recv_sem=recv1.at[o, c],
            device_id=(to, right), device_id_type=MESH)

    def send_right(c, o):
        to = lax.rem(right + o, rights)
        return pltpu.make_async_remote_copy(
            src_ref=second.at[pl.ds(c * step, step), pl.ds(pl.multiple_of(to * share_y, share_y), share_y), :],
            dst_ref=pencils.at[pl.ds(c * step, step), :, pl.ds(pl.multiple_of(right * width, width), width)],
            send_sem=send2.at[o, c], recv_sem=recv2.at[o, c],
            device_id=(left, to), device_id_type=MESH)

    def start1(c, carry):
        for o in range(1, lefts):
            send_left(c, o).start()
        return carry

    lax.fori_loop(0, chunks, start1, 0)

    def own1(x, carry):
        lines[:, pl.ds(x, 1), pl.ds(pl.multiple_of(left * own_y, own_y), own_y), :] = (
            first[:, pl.ds(left * share_x + x, 1)])
        return carry

    lax.fori_loop(0, share_x, own1, 0)
    copy_y.wait()
    copy_z.wait()

    pick = lax.broadcasted_iota(jnp.int32, (share_y, symbol_y.shape[1]), 1) == (
        right * share_y + lax.broadcasted_iota(jnp.int32, (share_y, symbol_y.shape[1]), 0))
    part_y = jnp.sum(jnp.where(pick, symbol_y[...], 0.0), axis=1, keepdims=True)
    modes_z = out.shape[2]

    def stage23(c, carry):
        @pl.when(c < chunks)
        def _():
            for o in range(1, lefts):
                send_left(c, o).wait_recv()
            for s in range(step):
                x = c * step + s
                values = jnp.concatenate([lines[b, x] for b in range(blocks)], axis=1)
                result = product((ty[0], ty[1]), split(values))
                second[x] = result
            for o in range(1, rights):
                send_right(c, o).start()
            for s in range(step):
                x = c * step + s
                pencils[x, :, pl.ds(pl.multiple_of(right * width, width), width)] = (
                    second[x, pl.ds(pl.multiple_of(right * share_y, share_y), share_y), :])

        @pl.when(c >= LAG)
        def _():
            d = c - LAG
            for o in range(1, rights):
                send_right(d, o).wait_recv()
            values = pencils[pl.ds(d * step, step)].reshape(step * share_y, pencils.shape[2])
            result = product(split(values), (tz[0], tz[1]))
            for s in range(step):
                x = d * step + s
                symbol = (symbol_x[left * share_x + x] + part_y) + symbol_z[:, :modes_z]
                out[x] = result[s * share_y : (s + 1) * share_y] * ((1.0 - 0.2 * symbol) / (1.0 + 0.2 * symbol))
        return carry

    lax.fori_loop(0, chunks + LAG, stage23, 0)

    def finish(c, carry):
        for o in range(1, lefts):
            send_left(c, o).wait_send()
        for o in range(1, rights):
            send_right(c, o).wait_send()
        return carry

    lax.fori_loop(0, chunks, finish, 0)


def body(lefts, rights, signal, symbol_x, symbol_y, symbol_z):
    size_x, own_y, own_z = signal.shape
    size_y, size_z = own_y * lefts, own_z * rights
    modes_x, modes_y, modes_z = size_x // 2, size_y // 2, size_z // 2
    share_x, share_y = modes_x // lefts, modes_y // rights
    chunks = min(8, share_x)
    blocks, tiles = own_z // LANES, own_y // ROWS
    table_x = two_halves(kept_table(size_x).T)
    table_y = two_halves(kept_table(size_y).T)
    table_z = two_halves(kept_table(size_z))
    vmem = pl.BlockSpec(memory_space=pltpu.VMEM)
    any_ = pl.BlockSpec(memory_space=pl.ANY)
    smem = pl.BlockSpec(memory_space=pltpu.SMEM)
    dma = pltpu.SemaphoreType.DMA
    return pl.pallas_call(
        functools.partial(kernel, lefts, rights, chunks),
        out_shape=jax.ShapeDtypeStruct((share_x, share_y, modes_z), jnp.float32),
        in_specs=[any_] * 4 + [smem, vmem, vmem],
        out_specs=vmem,
        scratch_shapes=[
            pltpu.VMEM((tiles, blocks, size_x, ROWS, LANES), jnp.float32),
            pltpu.VMEM(table_x.shape, jnp.bfloat16),
            pltpu.VMEM(table_y.shape, jnp.bfloat16),
            pltpu.VMEM(table_z.shape, jnp.bfloat16),
            pltpu.VMEM((blocks, modes_x, own_y, LANES), jnp.float32),
            pltpu.VMEM((blocks, share_x, size_y, LANES), jnp.float32),
            pltpu.VMEM((share_x, modes_y, own_z), jnp.float32),
            pltpu.VMEM((share_x, share_y, size_z), jnp.float32),
            dma((tiles, blocks)),
            dma((3,)),
            dma((lefts, chunks)),
            dma((lefts, chunks)),
            dma((rights, chunks)),
            dma((rights, chunks)),
        ],
        compiler_params=pltpu.CompilerParams(
            collective_id=0, has_side_effects=True, vmem_limit_bytes=62 * 2**20),
    )(signal, table_x, table_y, table_z, symbol_x, symbol_y[None, :], symbol_z[None, :])


def solution(mesh):
    lefts, rights = mesh.shape["left"], mesh.shape["right"]
    in_specs = (P(None, "left", "right"), P(), P(), P())
    out_specs = P("left", "right", None)
    return jax.shard_map(
        functools.partial(body, lefts, rights), mesh=mesh, in_specs=in_specs, out_specs=out_specs, check_vma=False)
```

time: 145 us -> 72.8 us (0.50)
  Pallas kernels: 0 us -> 70.3 us
  blocking collectives: 54 us -> 0 us
  waiting for transfers between devices: 30.7 us -> 0 us
  matrix products: 26.8 us -> 0 us
  other arithmetic: 17.8 us -> 0 us
  local copies, waits for them, and re-layouts: 10.4 us -> 2.29 us
  starting transfers between devices: 4.87 us -> 0 us
    pallas_call x0 -> x1, Pallas kernels: none -> 70.3 us  [body(): pl.pallas_call(functools.partial(kernel, lefts, rights, chunks), out_shap...]
    all_to_all x1 -> x0, blocking collectives: 54 us -> none  [body(): lax.all_to_all(part_values, 'left', split_axis=0, concat_axis=1, tiled=True)]
    all_to_all x1 -> x0, waiting for transfers between devices: 30.7 us -> none  [body(): lax.all_to_all(pencil_values, 'right', split_axis=1, concat_axis=2, tiled...]
    dot_general x3 -> x0, matrix products: 26.8 us -> none  [transform_dim(): jnp.tensordot(values, transform_table(values.shape[dim]), axes=([dim], [0...]
    mul x2 -> x0, other arithmetic: 17.7 us -> none  [transform_table(): return jnp.cos(angle) * (2.0 / count) ** 0.5]
    all_to_all x3 -> x0, local copies, waits for them, and re-layouts: 5.58 us -> none  [the longest x2 5 us: body(): lax.all_to_all(pencil_values, 'right', split_axis=1, concat_axis=2, tiled...]
    all_to_all x1 -> x0, starting transfers between devices: 4.87 us -> none  [body(): lax.all_to_all(pencil_values, 'right', split_axis=1, concat_axis=2, tiled...]
    slice x5 -> x0, local copies, waits for them, and re-layouts: 4.67 us -> none  [the longest x1 2.43 us: body(): lax.slice_in_dim(part_values, 0, part_values.shape[0] // 2, axis=0)]
  transfers between devices with their start and end apart: 1 -> 0, of which waited for: 1 -> 0; matrix products, arithmetic and copies ran while one was open for 12% -> 0% of each run, Pallas kernels for 0% -> 0%
where the time goes in v1:
time: 72.8 us; the launch traced here: 72.6 us
  Pallas kernels  70.3 us (97%)
  local copies, waits for them, and re-layouts  2.29 us (3%)
    pallas_call x1, Pallas kernels, body(): pl.pallas_call(functools.partial(kernel, lefts, rights, chunks), out_shap...  70.3 us
    unnamed x1, local copies, waits for them, and re-layouts  2.29 us

profile of v1, /device:TPU:0, one launch (start us, length us, event | category | flops | bytes accessed | tf_op | source)
XLA Modules:
  0.0 72.6 jit_solution(4552563031346358728)
XLA Ops:
  0.0 70.3 %shard_map.73 = f32[16,32,512]{2,1,0:T(8,128)} custom-call(f32[256,32,256]{2,1,0:T(8,128)} %signal.1, bf16[2,128,256]{2,1,0:T(8,128)(2,1)} %constant.4.clone.table_x.table_y, bf16[2,128,256]{2,1,0:T(8,128)(2,1)} %constant.4.clone.table_x.table_y, bf16[2,1024,512]{2,1,0:T(8,128)(2,1)} %constant.5.clone.table_z, f32[256]{0:T(256)} %symbol_x.1, ...), custom_call_target="tpu_custom_call" | custom-call | tf_op jit(solution)/shard_map/pallas_call | solution.py:186
  70.3 2.3 %copy.9 = f32[16,32,512]{2,1,0:T(8,128)} copy(f32[16,32,512]{2,1,0:T(8,128)} %shard_map.73) | data formatting | bytes 2097152

commit v2 on v1

--- a/solution.py
+++ b/solution.py
@@ -12,6 +12,7 @@
 LANES = 128
 ROWS = 8
 LAG = 2
+AHEAD = 2
 
 
 def kept_table(count):
@@ -41,12 +42,12 @@
     lefts, rights, chunks,
     signal, table_x, table_y, table_z, symbol_x, symbol_y, symbol_z, out,
     held, tx, ty, tz, first, lines, second, pencils,
-    held_sem, table_sem, send1, recv1, send2, recv2,
+    held_sem, table_sem, send0, recv0, send1, recv1, send2, recv2,
 ):
     left, right = lax.axis_index("left"), lax.axis_index("right")
     tiles, blocks, size_x = held.shape[0], held.shape[1], held.shape[2]
-    modes_x, own_y = first.shape[1], first.shape[2]
-    share_x, size_y = lines.shape[1], lines.shape[2]
+    modes_x, own_y = first.shape[0], first.shape[2]
+    share_x, size_y = lines.shape[1], lefts * own_y
     share_y = size_y // 2 // rights
     step = share_x // chunks
     width = blocks * LANES
@@ -60,11 +61,9 @@
     copy_y = pltpu.make_async_copy(table_y, ty, table_sem.at[1])
     copy_z = pltpu.make_async_copy(table_z, tz, table_sem.at[2])
     copy_x.start()
-    for t in range(tiles):
+    for t in range(min(AHEAD, tiles)):
         for b in range(blocks):
             tile_copy(t, b).start()
-    copy_y.start()
-    copy_z.start()
 
     barrier = pltpu.get_barrier_semaphore()
     for o in range(1, lefts):
@@ -74,48 +73,69 @@
 
     copy_x.wait()
 
+    def send_tile(t, o):
+        to = lax.rem(left + o, lefts)
+        return pltpu.make_async_remote_copy(
+            src_ref=first.at[pl.ds(to * share_x, step), :, pl.ds(pl.multiple_of(t * ROWS, ROWS), ROWS), :],
+            dst_ref=lines.at[left, pl.ds(0, step), :, pl.ds(pl.multiple_of(t * ROWS, ROWS), ROWS), :],
+            send_sem=send0.at[o, t], recv_sem=recv0.at[o, t],
+            device_id=(to, right), device_id_type=MESH)
+
+    def send_left(c, o):
+        to = lax.rem(left + o, lefts)
+        return pltpu.make_async_remote_copy(
+            src_ref=first.at[pl.ds(to * share_x + c * step, step)],
+            dst_ref=lines.at[left, pl.ds(c * step, step)],
+            send_sem=send1.at[o, c], recv_sem=recv1.at[o, c],
+            device_id=(to, right), device_id_type=MESH)
+
+    def send_right(c, o):
+        to = lax.rem(right + o, rights)
+        return pltpu.make_async_remote_copy(
+            src_ref=second.at[pl.ds(c * step, step), pl.ds(pl.multiple_of(to * share_y, share_y), share_y), :],
+            dst_ref=pencils.at[right, pl.ds(c * step, step)],
+            send_sem=send2.at[o, c], recv_sem=recv2.at[o, c],
+            device_id=(left, to), device_id_type=MESH)
+
     def stage1(t, carry):
         for b in range(blocks):
             tile_copy(t, b).wait()
+
+        @pl.when(t + AHEAD < tiles)
+        def _():
+            for b in range(blocks):
+                tile_copy(t + AHEAD, b).start()
+
         for y in range(ROWS):
             values = jnp.concatenate(
                 [held.at[t, b].reshape(size_x * ROWS, LANES)[pl.ds(y, size_x, stride=ROWS), :] for b in range(blocks)],
                 axis=1)
             result = product((tx[0], tx[1]), split(values))
             for b in range(blocks):
-                first.at[b].reshape(modes_x * own_y, LANES)[pl.ds(t * ROWS + y, modes_x, stride=own_y), :] = (
+                first.reshape(modes_x * blocks * own_y, LANES)[
+                    pl.ds(b * own_y + t * ROWS + y, modes_x, stride=blocks * own_y), :] = (
                     result[:, b * LANES : (b + 1) * LANES])
-        return carry
-
-    lax.fori_loop(0, tiles, stage1, 0)
-    pl.semaphore_wait(barrier, lefts + rights - 2)
-
-    def send_left(c, o):
-        to = lax.rem(left + o, lefts)
-        return pltpu.make_async_remote_copy(
-            src_ref=first.at[:, pl.ds(to * share_x + c * step, step)],
-            dst_ref=lines.at[:, pl.ds(c * step, step), pl.ds(pl.multiple_of(left * own_y, own_y), own_y), :],
-            send_sem=send1.at[o, c], recv_sem=recv1.at[o, c],
-            device_id=(to, right), device_id_type=MESH)
-
-    def send_right(c, o):
-        to = lax.rem(right + o, rights)
-        return pltpu.make_async_remote_copy(
-            src_ref=second.at[pl.ds(c * step, step), pl.ds(pl.multiple_of(to * share_y, share_y), share_y), :],
-            dst_ref=pencils.at[pl.ds(c * step, step), :, pl.ds(pl.multiple_of(right * width, width), width)],
-            send_sem=send2.at[o, c], recv_sem=recv2.at[o, c],
-            device_id=(left, to), device_id_type=MESH)
+
+        @pl.when(t == 0)
+        def _():
+            pl.semaphore_wait(barrier, lefts + rights - 2)
+
+        for o in range(1, lefts):
+            send_tile(t, o).start()
+        return carry
 
     def start1(c, carry):
         for o in range(1, lefts):
             send_left(c, o).start()
         return carry
 
-    lax.fori_loop(0, chunks, start1, 0)
+    lax.fori_loop(0, tiles, stage1, 0)
+    lax.fori_loop(1, chunks, start1, 0)
+    copy_y.start()
+    copy_z.start()
 
     def own1(x, carry):
-        lines[:, pl.ds(x, 1), pl.ds(pl.multiple_of(left * own_y, own_y), own_y), :] = (
-            first[:, pl.ds(left * share_x + x, 1)])
+        lines[left, x] = first[left * share_x + x]
         return carry
 
     lax.fori_loop(0, share_x, own1, 0)
@@ -130,26 +150,35 @@
     def stage23(c, carry):
         @pl.when(c < chunks)
         def _():
-            for o in range(1, lefts):
-                send_left(c, o).wait_recv()
+            @pl.when(c == 0)
+            def _():
+                for t in range(tiles):
+                    for o in range(1, lefts):
+                        send_tile(t, o).wait_recv()
+
+            @pl.when(c > 0)
+            def _():
+                for o in range(1, lefts):
+                    send_left(c, o).wait_recv()
+
             for s in range(step):
                 x = c * step + s
-                values = jnp.concatenate([lines[b, x] for b in range(blocks)], axis=1)
+                values = jnp.concatenate([lines[:, x, b].reshape(size_y, LANES) for b in range(blocks)], axis=1)
                 result = product((ty[0], ty[1]), split(values))
                 second[x] = result
             for o in range(1, rights):
                 send_right(c, o).start()
             for s in range(step):
                 x = c * step + s
-                pencils[x, :, pl.ds(pl.multiple_of(right * width, width), width)] = (
-                    second[x, pl.ds(pl.multiple_of(right * share_y, share_y), share_y), :])
+                pencils[right, x] = second[x, pl.ds(pl.multiple_of(right * share_y, share_y), share_y), :]
 
         @pl.when(c >= LAG)
         def _():
             d = c - LAG
             for o in range(1, rights):
                 send_right(d, o).wait_recv()
-            values = pencils[pl.ds(d * step, step)].reshape(step * share_y, pencils.shape[2])
+            values = jnp.concatenate(
+                [pencils[p, pl.ds(d * step, step)].reshape(step * share_y, width) for p in range(rights)], axis=1)
             result = product(split(values), (tz[0], tz[1]))
             for s in range(step):
                 x = d * step + s
@@ -160,11 +189,18 @@
     lax.fori_loop(0, chunks + LAG, stage23, 0)
 
     def finish(c, carry):
-        for o in range(1, lefts):
-            send_left(c, o).wait_send()
+        @pl.when(c > 0)
+        def _():
+            for o in range(1, lefts):
+                send_left(c, o).wait_send()
+
         for o in range(1, rights):
             send_right(c, o).wait_send()
         return carry
+
+    for t in range(tiles):
+        for o in range(1, lefts):
+            send_tile(t, o).wait_send()
 
     lax.fori_loop(0, chunks, finish, 0)
 
@@ -193,12 +229,14 @@
             pltpu.VMEM(table_x.shape, jnp.bfloat16),
             pltpu.VMEM(table_y.shape, jnp.bfloat16),
             pltpu.VMEM(table_z.shape, jnp.bfloat16),
-            pltpu.VMEM((blocks, modes_x, own_y, LANES), jnp.float32),
-            pltpu.VMEM((blocks, share_x, size_y, LANES), jnp.float32),
+            pltpu.VMEM((modes_x, blocks, own_y, LANES), jnp.float32),
+            pltpu.VMEM((lefts, share_x, blocks, own_y, LANES), jnp.float32),
             pltpu.VMEM((share_x, modes_y, own_z), jnp.float32),
-            pltpu.VMEM((share_x, share_y, size_z), jnp.float32),
+            pltpu.VMEM((rights, share_x, share_y, own_z), jnp.float32),
             dma((tiles, blocks)),
             dma((3,)),
+            dma((lefts, tiles)),
+            dma((lefts, tiles)),
             dma((lefts, chunks)),
             dma((lefts, chunks)),
             dma((rights, chunks)),

time: 72.8 us -> 69 us (0.948)
  Pallas kernels: 70.3 us -> 66.4 us
    pallas_call x1, Pallas kernels: 70.3 us -> 66.4 us  [body(): pl.pallas_call(functools.partial(kernel, lefts, rights, chunks), out_shap...]
where the time goes in v2:
time: 69 us; the launch traced here: 68.7 us
  Pallas kernels  66.4 us (96%)
  local copies, waits for them, and re-layouts  2.29 us (3%)
    pallas_call x1, Pallas kernels, body(): pl.pallas_call(functools.partial(kernel, lefts, rights, chunks), out_shap...  66.4 us
    unnamed x1, local copies, waits for them, and re-layouts  2.29 us

profile of v2, /device:TPU:0, one launch (start us, length us, event | category | flops | bytes accessed | tf_op | source)
XLA Modules:
  0.0 68.7 jit_solution(15798120360994047970)
XLA Ops:
  0.0 66.4 %shard_map.73 = f32[16,32,512]{2,1,0:T(8,128)} custom-call(f32[256,32,256]{2,1,0:T(8,128)} %signal.1, bf16[2,128,256]{2,1,0:T(8,128)(2,1)} %constant.4.clone.table_x.table_y, bf16[2,128,256]{2,1,0:T(8,128)(2,1)} %constant.4.clone.table_x.table_y, bf16[2,1024,512]{2,1,0:T(8,128)(2,1)} %constant.5.clone.table_z, f32[256]{0:T(256)} %symbol_x.1, ...), custom_call_target="tpu_custom_call" | custom-call | tf_op jit(solution)/shard_map/pallas_call | solution.py:222
  66.4 2.3 %copy.9 = f32[16,32,512]{2,1,0:T(8,128)} copy(f32[16,32,512]{2,1,0:T(8,128)} %shard_map.73) | data formatting | bytes 2097152
